TPU v7x, 512 devices: a whole 4x4x16 slice. The times are simulated.
512 devices in a mesh: seq: 32 (over z, core), head: 16 (over y, x).
Axes of the slice: x: 4, y: 4, z: 16, core: 2. Of those that a mesh axis runs over, the one named last changes fastest.
Arguments:
- queries: bfloat16 [65536, 16, 128], P(('seq', 'head')), may hold values from -6 to 6
- keys: bfloat16 [65536, 16, 128], P(('seq', 'head')), may hold values from -6 to 6
- values: bfloat16 [65536, 16, 128], P(('seq', 'head')), may hold values from -6 to 6
- beta: float32 [65536, 16], P(('seq', 'head')), may hold values from 0 to 1
- log_decay: float32 [65536, 16], P(('seq', 'head')), may hold values from -1 to 0
- out_gate: bfloat16 [65536, 16, 128], P(('seq', 'head')), may hold values from -6 to 6
- norm_gain: float32 [128], replicated, may hold values from 0.1 to 1.9
Outputs:
- gated_out: bfloat16 [65536, 16, 128], P('seq', 'head')
All inputs are finite; a program needn't handle non-finite values.
Results may differ from a plain program's by a relative error of at most 0.001.
Values may be sent and summed in bfloat16 or wider, within the bound.
No kernel may reach another device: no remote copies, remote signals or barrier semaphores. Data moves between devices by JAX's collectives and lax.ppermute only.
A program may use at most 64 MiB of HBM per device.

v0:
```python
import jax
import jax.numpy as jnp
from jax import lax
from jax.experimental import pallas as pl
from jax.experimental.pallas import tpu as pltpu
from jax.sharding import Mesh
from jax.sharding import PartitionSpec as P


F32 = jnp.float32
BF16 = jnp.bfloat16
N = 128
EPS = 1e-06
SUB = 16


def dot(a, b):
    return jnp.dot(a, b, preferred_element_type=F32)


def dot_nt(a, b):
    return lax.dot_general(a, b, (((1,), (1,)), ((), ())), preferred_element_type=F32)


def split2(x):
    high = x.astype(BF16)
    return high, (x - high.astype(F32)).astype(BF16)


def lanes(*parts):
    return jnp.concatenate(parts, axis=1)


def rows(*parts):
    return jnp.concatenate(parts, axis=0)


def square_mm(a_parts, b_parts):
    b_both = lanes(*b_parts)
    both = dot(lanes(*a_parts), rows(b_both, b_both))
    return both[:, :N] + both[:, N:]


def wide_mm(a_parts, b_high, b_low):
    return dot(lanes(*a_parts), rows(b_high, b_high)) + dot(a_parts[0], b_low)


def compose(later, earlier):
    high, low = split2(earlier)
    out = wide_mm(split2(later[:, :N]), high, low)
    return out + lanes(jnp.zeros((N, N), F32), later[:, N:])


def iotas():
    return lax.broadcasted_iota(jnp.int32, (N, N), 0), lax.broadcasted_iota(jnp.int32, (N, N), 1)


def terms_kernel(core_ref, kv_ref, map_ref, off_ref, send_ref, *rest):
    outs, (en_ref, grow_ref, wu_hi_ref, wu_lo_ref, node_ref), sems = rest[:5], rest[5:10], rest[10]
    blocks = kv_ref.shape[0]
    copies = []

    def save(which, first=0, count=blocks):
        part = pl.ds(first, count)
        copies.append(
            pltpu.make_async_copy(rest[5 + which].at[part], outs[which].at[part], sems.at[len(copies)])
        )
        copies[-1].start()

    r, c = iotas()
    one = lambda cond: cond.astype(F32).astype(BF16)
    lower = one(r >= c)
    eye16 = one(r == c)
    eye = (r == c).astype(F32)
    inclusive = r >= c
    picks = lanes(one(r > c), jnp.ones((N, N), BF16))
    picks = rows(picks, picks, picks)
    lane16 = lax.broadcasted_iota(jnp.int32, (SUB, N), 1)
    row16 = lax.broadcasted_iota(jnp.int32, (SUB, N), 0)
    start16 = (row16 == lane16 % SUB).astype(F32)
    base16 = lane16 // SUB * SUB
    merge_masks = [one((r // m == c // m + 1) & (c // m % 2 == 0)) for m in (16, 32, 64)]
    group = range(blocks)

    keys = [kv_ref[b, :N, :N] for b in group]
    kk = [dot_nt(k, k) for k in keys]
    aux = [kv_ref[b, N : N + 8, :] for b in group]

    def sums(a):
        left = [rows(lower * a[i : i + 1, :N], eye16 * a[i : i + 1, N:]) for i in range(3)]
        return dot(lanes(*left), picks)

    summed = [sums(a) for a in aux]
    fade = [jnp.exp(s[:N, :N]) for s in summed]
    cum = [s[:N, N:] for s in summed]
    beta_low = [s[N:, :N] for s in summed]
    beta_row = []
    cum_row = []
    for b in group:
        a = aux[b][:8].astype(F32)
        beta_row.append(a[0:1, N:] + a[1:2, N:] + a[2:3, N:])
        cum_row.append(jnp.sum(eye * cum[b], axis=0, keepdims=True))
    diag = [eye * x for x in kk]
    nk_row = [lax.rsqrt(jnp.sum(d, axis=0, keepdims=True) + EPS) for d in diag]
    nk_col = [lax.rsqrt(jnp.sum(d, axis=1, keepdims=True) + EPS) for d in diag]
    low = []
    for b in group:
        fade_n = fade[b] * nk_row[b]
        en_ref[b] = jnp.where(inclusive, fade_n, 0.0)
        low.append(beta_low[b] * fade_n * (nk_col[b] * kk[b]))
        grow_ref[b] = jnp.exp(cum[b])
    save(0)
    save(1)
    inv = []
    for b in group:
        small = sum(
            jnp.where(lane16 // SUB == s, low[b][SUB * s : SUB * (s + 1)], 0.0) for s in range(N // SUB)
        )
        x = start16
        for j in range(SUB - 1):
            col = jnp.take_along_axis(small, base16 + j, axis=1)
            x = x - col * x[j : j + 1, :]
        inv.append(rows(*[jnp.where(lane16 // SUB == s, x, 0.0) for s in range(N // SUB)]))
    low_parts = [split2(x) for x in low]
    for mask in merge_masks:
        parts = [split2(x) for x in inv]
        left = [square_mm(parts[b], [p * mask for p in low_parts[b]]) for b in group]
        left = [split2(x) for x in left]
        inv = [inv[b] - square_mm(left[b], parts[b]) for b in group]
    pairs = []
    for b in group:
        grow_row = jnp.exp(cum_row[b])
        for_u = inv[b] * beta_row[b]
        for_w = for_u * (grow_row * nk_row[b])
        value = kv_ref[b, :N, N:]
        w = dot(lanes(*split2(for_w)), rows(keys[b], keys[b]))
        u = dot(lanes(*split2(for_u)), rows(value, value))
        wu = lanes(w, u)
        wu_hi_ref[b], wu_lo_ref[b] = split2(wu)
        total = cum[b][N - 1 : N, :]
        tail = jnp.exp(total - cum[b]) * nk_col[b]
        high, lo = split2(wu * lanes(tail, tail))
        key_t = keys[b].T
        out = dot(lanes(key_t, key_t), rows(high, lo))
        pair = lanes(eye * jnp.exp(total) - out[:, :N], out[:, N:])
        node_ref[b] = pair
        pairs.append(pair)
    save(2)
    save(3)
    save(4)
    spot = blocks
    while len(pairs) > 2:
        pairs = [compose(pairs[i + 1], pairs[i]) for i in range(0, len(pairs), 2)]
        for i, pair in enumerate(pairs):
            node_ref[spot + i] = pair
        save(4, spot, len(pairs))
        spot += len(pairs)
    total = compose(pairs[1], pairs[0])
    map_ref[...] = total[:, :N]
    off_ref[...] = total[:, N:]
    send_ref[...] = jnp.where(core_ref[0] == 0, total[:, N:], total[:, :N])
    for copy in copies:
        copy.wait()


def reach_kernel(kv_ref, q_ref, *rest):
    sources, (r0_ref, hi_ref, lo_ref) = rest[:5], rest[5:8]
    buffers, sems = rest[8:13], rest[13]
    blocks = kv_ref.shape[0]
    copies = [
        pltpu.make_async_copy(sources[i], buffers[i], sems.at[i]) for i in range(len(sources))
    ]
    for copy in copies:
        copy.start()
    node_ref, en_ref, grow_ref, wu_hi_ref, wu_lo_ref = buffers
    copies[0].wait()
    carried = {}
    base, width = {1: 0}, 1
    while width * 2 < blocks:
        base[width * 2] = base[width] + blocks // width
        width *= 2
    step = blocks // 2
    while step:
        for b in range(step, blocks, 2 * step):
            node = node_ref[base[step] + (b - step) // step]
            carried[b] = compose(node, carried[b - step]) if b > step else node
        step //= 2
    for copy in copies[1:]:
        copy.wait()
    for b in range(blocks):
        q = q_ref[b, :, :N]
        mixing = en_ref[b] * dot_nt(q, kv_ref[b, :N, :N])
        mixed = wide_mm(split2(mixing), wu_hi_ref[b], wu_lo_ref[b])
        q32 = q.astype(F32)
        scale = lax.rsqrt(jnp.sum(q32 * q32, axis=1, keepdims=True) + EPS) * N**-0.5
        reach = grow_ref[b] * q32 - mixed[:, :N]
        local = mixed[:, N:]
        if b:
            high, low = split2(carried[b])
            out = wide_mm(split2(reach), high, low)
            reach, local = out[:, :N], local + out[:, N:]
        r0_ref[b] = local * scale
        hi_ref[b], lo_ref[b] = split2(reach * scale)


def advance(left, right, extra):
    return square_mm(split2(left), split2(right)) + extra


def pair_kernel(core_ref, map_ref, off_ref, got_ref, out_ref):
    first = core_ref[0] == 0
    own = map_ref[...]
    got = got_ref[...]
    left = jnp.where(first, got, own)
    right = jnp.where(first, own, got)
    out_ref[...] = advance(left, right, jnp.where(first, 0.0, off_ref[...]))


def join_kernel(core_ref, near_ref, map_ref, far_ref, out_ref):
    first = core_ref[0] == 0
    near = near_ref[...]
    left = jnp.where(first, near, map_ref[...])
    out_ref[...] = advance(left, far_ref[...], jnp.where(first, 0.0, near))


def finish_kernel(core_ref, r0_ref, hi_ref, lo_ref, own_ref, swap_ref, far0_ref, far1_ref, map_ref, off_ref, gate_ref, gain_ref, out_ref):
    first = core_ref[0] == 0
    own = own_ref[...]
    swap = swap_ref[...]
    state = advance(
        jnp.where(first, own, swap), far0_ref[...] + far1_ref[...], jnp.where(first, swap, own)
    )
    state = jnp.where(first, state, advance(map_ref[...], state, off_ref[...]))
    y_both = lanes(*split2(state))
    y_both = rows(y_both, y_both)
    for b in range(r0_ref.shape[0]):
        both = dot(lanes(hi_ref[b], lo_ref[b]), y_both)
        res = r0_ref[b] + both[:, :N] + both[:, N:]
        norm = lax.rsqrt(jnp.mean(res * res, axis=1, keepdims=True) + EPS)
        gate = gate_ref[b, :, N:].astype(F32)
        silu = gate / (1.0 + jnp.exp(-gate))
        out_ref[b] = (res * norm * gain_ref[...] * silu).astype(BF16)


def call(kernel, out_shape, inputs, core=None, remote=(), spill=(), sems=0):
    vmem = pl.BlockSpec(memory_space=pltpu.VMEM)
    hbm = pl.BlockSpec(memory_space=pltpu.HBM)
    specs = [vmem] * len(inputs) + [hbm] * len(remote)
    inputs = [*inputs, *(pltpu.with_memory_space_constraint(a, pltpu.HBM) for a in remote)]
    if core is not None:
        specs = [pl.BlockSpec(memory_space=pltpu.SMEM)] + specs
        inputs = [core, *inputs]
    return pl.pallas_call(
        kernel,
        out_shape=[*out_shape, *(pltpu.HBM(o.shape, o.dtype) for o in spill)],
        in_specs=specs,
        out_specs=[vmem] * len(out_shape) + [hbm] * len(spill),
        scratch_shapes=[pltpu.VMEM(o.shape, o.dtype) for o in (*remote, *spill)]
        + ([pltpu.SemaphoreType.DMA((sems,))] if sems else []),
        compiler_params=pltpu.CompilerParams(vmem_limit_bytes=40 * 2**20),
    )(*inputs)


def near(*arrays):
    return [pltpu.with_memory_space_constraint(a, pltpu.VMEM) for a in arrays]


def kept(*dims, dtype=F32):
    return pltpu.VMEM(dims, dtype)


def shape(*dims, dtype=F32):
    return jax.ShapeDtypeStruct(dims, dtype)


def parts3(x):
    high = lax.reduce_precision(x, 8, 7)
    rest = x - high
    mid = lax.reduce_precision(rest, 8, 7)
    return [p.astype(BF16) for p in (high, mid, rest - mid)]


def by_head(array):
    return jnp.transpose(array, (1, 0, 2))


def to_heads(array):
    return lax.all_to_all(array, "head", split_axis=0, concat_axis=0, tiled=True)


def layer(queries, keys, values, beta, log_decay, out_gate, norm_gain):
    z = lax.axis_size("z")
    decay_parts = parts3(jnp.transpose(log_decay))
    beta_parts = parts3(jnp.transpose(beta))
    aux = jnp.concatenate(
        [jnp.stack(decay_parts, axis=1), jnp.stack(beta_parts, axis=1)], axis=2
    )
    aux = jnp.pad(aux, ((0, 0), (0, 5), (0, 0)))
    kv = jnp.concatenate([by_head(keys), by_head(values)], axis=2)
    kv = to_heads(jnp.concatenate([kv, aux], axis=1))
    qg = jnp.concatenate([by_head(queries), by_head(out_gate)], axis=2)
    blocks = kv.shape[0]
    cube = shape(blocks, N, N)
    square = kept(N, N)
    wide16 = shape(blocks, N, 2 * N, dtype=BF16)
    core = lax.axis_index("c").astype(jnp.int32).reshape(1)
    kv, qg = lax.optimization_barrier((kv, qg))
    own_map, own_off, send, en, grow, wu_hi, wu_lo, nodes = call(
        terms_kernel,
        [square] * 3,
        near(kv),
        core,
        spill=[cube, cube, wide16, wide16, shape(2 * blocks - 2, N, 2 * N)],
        sems=8,
    )
    swap = [(0, 1), (1, 0)]
    got = lax.ppermute(send, "c", swap)
    first_map = lax.ppermute(own_map, "c", [(0, 1)])
    chip = call(pair_kernel, [square], near(own_map, own_off, got), core)[0]

    def up(x, d):
        return lax.ppermute(x, "z", [(i, i + d) for i in range(z - d)])

    def cross(x, d, *routes):
        pairs = [
            (2 * i + source, 2 * (i + d) + target)
            for i in range(z - d)
            for source, target in zip(routes[::2], routes[1::2])
        ]
        return lax.ppermute(x, ("z", "c"), pairs)

    def join(one, maps, far):
        return call(join_kernel, [square], near(one, maps, far), core)[0]

    window, span = chip, 1
    while span * 2 < z:
        far = up(window, span)
        maps = lax.ppermute(window, "c", [(0, 1)])
        if span * 4 >= z:
            qg, maps = lax.optimization_barrier((qg, maps))
            qg = to_heads(qg)
        window = join(window, maps, far)
        span *= 2
    qg, window = lax.optimization_barrier((qg, window))
    far0 = cross(window, span + 1, 1, 0)
    far1 = cross(window, span + 1, 1, 1)
    own = up(window, 1)
    other = cross(window, 1, 0, 1, 1, 0)
    half = kept(blocks, N, N, dtype=BF16)
    r0, r1_hi, r1_lo = call(
        reach_kernel,
        [kept(blocks, N, N), half, half],
        near(kv, qg),
        remote=[nodes, en, grow, wu_hi, wu_lo],
        sems=5,
    )
    (out,) = call(
        finish_kernel,
        [shape(blocks, N, N, dtype=BF16)],
        near(r0, r1_hi, r1_lo, own, other, far0, far1, first_map, got)
        + [qg, norm_gain.reshape(1, N)],
        core,
    )
    return out.reshape(blocks * N, 1, N)


def solution(mesh):
    finer = Mesh(mesh.devices.reshape(-1, 2, mesh.shape["head"]), ("z", "c", "head"))
    tokens = ("z", "c", "head")
    in_specs = (
        P(tokens, None, None),
        P(tokens, None, None),
        P(tokens, None, None),
        P(tokens, None),
        P(tokens, None),
        P(tokens, None, None),
        P(),
    )
    out_specs = P(("z", "c"), "head", None)
    return jax.shard_map(layer, mesh=finer, in_specs=in_specs, out_specs=out_specs, check_vma=False)
```

profile of v0, /device:TPU:32, one launch (start us, length us, event | category | flops | bytes accessed | tf_op | source)
XLA Modules:
  0.0 113.2 jit_solution(17518024839952571471)
XLA Ops:
  0.7 0.7 fusion.15
  1.5 1.5 %copy_bitcast_fusion.2 = (bf16[16,128,128]{2,1,0:T(8,128)(2,1)S(1)}, bf16[16,128,128]{2,1,0:T(8,128)(2,1)S(1)}) fusion(bf16[128,16,128]{2,1,0:T(8,128)(2,1)} %param.9, bf16[128,16,128]{2,1,0:T(8,128)(2,1)} %param.8), kind=kLoop, calls=%fused_computation.4 | loop fusion | bytes 2097152 | tf_op jit(solution)/shard_map/transpose | solution.py:284
  3.1 1.2 %pad_maximum_fusion = bf16[16,136,256]{2,1,0:T(8,128)(2,1)} fusion(bf16[16,8,256]{2,1,0:T(8,128)(2,1)S(1)} %fusion.8, bf16[16,128,128]{2,1,0:T(8,128)(2,1)S(1)} %get-tuple-element.45, bf16[16,128,128]{2,1,0:T(8,128)(2,1)S(1)} %get-tuple-element.46), kind=kLoop, calls=%fused_computation | loop fusion | flops 3342336 | bytes 2228224 | tf_op jit(solution)/shard_map/concatenate | solution.py:300
  4.2 7.0 %all-to-all-start = ((bf16[16,136,256]{2,1,0:T(8,128)(2,1)}), bf16[16,136,256]{2,1,0:T(8,128)(2,1)S(1)}, u32[]{:S(2)}, u32[]{:S(2)}) async-start(bf16[16,136,256]{2,1,0:T(8,128)(2,1)} %pad_maximum_fusion), calls=%async_computation | async-start | bytes 2228224 | tf_op jit(solution)/shard_map/all_to_all | solution.py:288
  11.6 1.1 pad_maximum_fusion.1
  12.7 17.0 %all-to-all-done.kv_ref = bf16[16,136,256]{2,1,0:T(8,128)(2,1)S(1)} async-done(((bf16[16,136,256]{2,1,0:T(8,128)(2,1)}), bf16[16,136,256]{2,1,0:T(8,128)(2,1)S(1)}, u32[]{:S(2)}, u32[]{:S(2)}) %all-to-all-start) | async-done | bytes 1114144 | tf_op jit(solution)/shard_map/all_to_all | solution.py:288
  29.7 10.1 %shard_map.73 = (f32[128,128]{1,0:T(8,128)S(1)}, f32[128,128]{1,0:T(8,128)S(1)}, f32[128,128]{1,0:T(8,128)S(1)}, f32[16,128,128]{2,1,0:T(8,128)}, f32[16,128,128...) custom-call(s32[1]{0:T(128)} %bitcast.core_ref, ...), custom_call_target="tpu_custom_call" | custom-call | tf_op jit(solution)/shard_map/pallas_call | solution.py:253
  39.9 1.9 %collective-permute-start = (f32[128,128]{1,0:T(8,128)S(1)}, f32[128,128]{1,0:T(8,128)S(1)}, u32[]{:S(2)}, u32[]{:S(2)}) collective-permute-start(f32[128,128]{1,0:T(8,128)S(1)} %get-tuple-element.26), channel_id=1, source_target_pairs={{0,16},{16,0},{1,17},{17,1},{2,18},{18,2},{3,19},{19,3},{4,20},{20... | collective-permute-start | bytes 196616 | tf_op jit(solution)/shard_map/ppermute | solution.py:317
  41.8 1.2 %collective-permute-done.got_ref.off_ref = f32[128,128]{1,0:T(8,128)S(1)} collective-permute-done((f32[128,128]{1,0:T(8,128)S(1)}, f32[128,128]{1,0:T(8,128)S(1)}, u32[]{:S(2)}, u32[]{:S(2)}) %collective-permute-start) | collective-permute-done | bytes 65568 | tf_op jit(solution)/shard_map/ppermute | solution.py:317
  43.2 3.8 %collective-permute-start.2 = (f32[128,128]{1,0:T(8,128)S(1)}, f32[128,128]{1,0:T(8,128)S(1)}, u32[]{:S(2)}, u32[]{:S(2)}) collective-permute-start(f32[128,128]{1,0:T(8,128)S(1)} %shard_map.74.near_ref), channel_id=1, source_target_pairs={{0,32},{32,64},{64,96},{96,128},{128,160},{160,192},{192,224},{224... | collective-permute-start | bytes 196616 | tf_op jit(solution)/shard_map/ppermute | solution.py:322
  47.1 1.8 %collective-permute-start.1 = (f32[128,128]{1,0:T(8,128)S(1)}, f32[128,128]{1,0:T(8,128)S(1)}, u32[]{:S(2)}, u32[]{:S(2)}) collective-permute-start(f32[128,128]{1,0:T(8,128)S(1)} %shard_map.74.near_ref), channel_id=1, source_target_pairs={{0,16},{1,17},{2,18},{3,19},{4,20},{5,21},{6,22},{7,23},{8,24},{9,... | collective-permute-start | bytes 196616 | tf_op jit(solution)/shard_map/ppermute | solution.py:338
  49.9 6.4 %collective-permute-start.4 = (f32[128,128]{1,0:T(8,128)S(1)}, f32[128,128]{1,0:T(8,128)S(1)}, u32[]{:S(2)}, u32[]{:S(2)}) collective-permute-start(f32[128,128]{1,0:T(8,128)S(1)} %shard_map.75.near_ref), channel_id=1, source_target_pairs={{0,64},{32,96},{64,128},{96,160},{128,192},{160,224},{192,256},{22... | collective-permute-start | bytes 196616 | tf_op jit(solution)/shard_map/ppermute | solution.py:322
  56.3 2.0 %collective-permute-start.3 = (f32[128,128]{1,0:T(8,128)S(1)}, f32[128,128]{1,0:T(8,128)S(1)}, u32[]{:S(2)}, u32[]{:S(2)}) collective-permute-start(f32[128,128]{1,0:T(8,128)S(1)} %shard_map.75.near_ref), channel_id=1, source_target_pairs={{0,16},{1,17},{2,18},{3,19},{4,20},{5,21},{6,22},{7,23},{8,24},{9,... | collective-permute-start | bytes 196616 | tf_op jit(solution)/shard_map/ppermute | solution.py:338
  58.3 0.9 collective-permute-done.3.map_ref
  59.3 2.3 %collective-permute-start.5 = (f32[128,128]{1,0:T(8,128)S(1)}, f32[128,128]{1,0:T(8,128)S(1)}, u32[]{:S(2)}, u32[]{:S(2)}) collective-permute-start(f32[128,128]{1,0:T(8,128)S(1)} %shard_map.76.near_ref), channel_id=1, source_target_pairs={{0,16},{1,17},{2,18},{3,19},{4,20},{5,21},{6,22},{7,23},{8,24},{9,... | collective-permute-start | bytes 196616 | tf_op jit(solution)/shard_map/ppermute | solution.py:338
  61.6 0.9 collective-permute-done.5.map_ref
  62.5 3.7 %all-to-all-start.1 = ((bf16[16,128,256]{2,1,0:T(8,128)(2,1)}), bf16[16,128,256]{2,1,0:T(8,128)(2,1)S(1)}, u32[]{:S(2)}, u32[]{:S(2)}) async-start(bf16[16,128,256]{2,1,0:T(8,128)(2,1)} %pad_maximum_fusion.1), calls=%async_computation.1 | async-start | bytes 2097152 | tf_op jit(solution)/shard_map/all_to_all | solution.py:288
  66.1 9.1 %collective-permute-start.6 = (f32[128,128]{1,0:T(8,128)S(1)}, f32[128,128]{1,0:T(8,128)S(1)}, u32[]{:S(2)}, u32[]{:S(2)}) collective-permute-start(f32[128,128]{1,0:T(8,128)S(1)} %shard_map.76.near_ref), channel_id=1, source_target_pairs={{0,128},{32,160},{64,192},{96,224},{128,256},{160,288},{192,320},{... | collective-permute-start | bytes 196616 | tf_op jit(solution)/shard_map/ppermute | solution.py:322
  75.2 2.0 %collective-permute-start.11 = (f32[128,128]{1,0:T(8,128)S(1)}, f32[128,128]{1,0:T(8,128)S(1)}, u32[]{:S(2)}, u32[]{:S(2)}) collective-permute-start(f32[128,128]{1,0:T(8,128)S(1)} %get-tuple-element.24.map_ref), channel_id=1, source_target_pairs={{0,16},{1,17},{2,18},{3,19},{4,20},{5,21},{6,22},{7,23},{8,24},{9,... | collective-permute-start | bytes 196616 | tf_op jit(solution)/shard_map/ppermute | solution.py:318
  77.5 7.7 %all-to-all-done.1.q_ref.gate_ref = bf16[16,128,256]{2,1,0:T(8,128)(2,1)S(1)} async-done(((bf16[16,128,256]{2,1,0:T(8,128)(2,1)}), bf16[16,128,256]{2,1,0:T(8,128)(2,1)S(1)}, u32[]{:S(2)}, u32[]{:S(2)}) %all-to-all-start.1) | async-done | bytes 1048608 | tf_op jit(solution)/shard_map/all_to_all | solution.py:288
  86.5 13.7 %collective-permute-start.8 = (f32[128,128]{1,0:T(8,128)S(1)}, f32[128,128]{1,0:T(8,128)S(1)}, u32[]{:S(2)}, u32[]{:S(2)}) collective-permute-start(f32[128,128]{1,0:T(8,128)S(1)} %shard_map.77), channel_id=1, source_target_pairs={{0,48},{16,32},{32,80},{48,64},{64,112},{80,96},{96,144},{112,128}... | collective-permute-start | bytes 196616 | tf_op jit(solution)/shard_map/ppermute | solution.py:330
  100.2 4.0 %collective-permute-start.7 = (f32[128,128]{1,0:T(8,128)S(1)}, f32[128,128]{1,0:T(8,128)S(1)}, u32[]{:S(2)}, u32[]{:S(2)}) collective-permute-start(f32[128,128]{1,0:T(8,128)S(1)} %shard_map.77), channel_id=1, source_target_pairs={{0,32},{32,64},{64,96},{96,128},{128,160},{160,192},{192,224},{224... | collective-permute-start | bytes 196616 | tf_op jit(solution)/shard_map/ppermute | solution.py:322
  104.2 7.0 %shard_map.78 = (f32[16,128,128]{2,1,0:T(8,128)S(1)}, bf16[16,128,128]{2,1,0:T(8,128)(2,1)S(1)}, bf16[16,128,128]{2,1,0:T(8,128)(2,1)S(1)}) custom-call(bf16[16,136,256]{2,1,0:T(8,128)(2,1)S(1)} %all-to-all-done.kv_ref, bf16[16,128,256]{2,1,0:T(8,128)(2,1)S(1)} %all-to-all-done.1.q_ref.gate_ref, f32[30,128,256]{2,1,0:T(8,128)} %get-tuple-element.30.rest_0_, ...), custom_call_target="tpu_custom_call" | custom-call | tf_op jit(solution)/shard_map/pallas_call | solution.py:253
  111.3 1.9 %shard_map.79 = bf16[16,128,128]{2,1,0:T(8,128)(2,1)} custom-call(s32[1]{0:T(128)} %bitcast.core_ref, f32[16,128,128]{2,1,0:T(8,128)S(1)} %get-tuple-element.35.r0_ref, bf16[16,128,128]{2,1,0:T(8,128)(2,1)S(1)} %get-tuple-element.36.hi_ref, bf16[16,128,128]{2,1,0:T(8,128)(2,1)S(1)} %get-tuple-element.37.lo_ref, ...), custom_call_target="tpu_custom_call" | custom-call | tf_op jit(solution)/shard_map/pallas_call | solution.py:253
  (30 shorter events, 4.1 us)
Async XLA Ops:
  3.1 8.2 %copy-start.1 = (bf16[128,16,128]{2,1,0:T(8,128)(2,1)S(1)}, bf16[128,16,128]{2,1,0:T(8,128)(2,1)}, u32[]{:S(2)}) copy-start(bf16[128,16,128]{2,1,0:T(8,128)(2,1)} %param.12) | copy-start | bytes 1572868
  3.1 8.2 %copy-start.2 = (bf16[128,16,128]{2,1,0:T(8,128)(2,1)S(1)}, bf16[128,16,128]{2,1,0:T(8,128)(2,1)}, u32[]{:S(2)}) copy-start(bf16[128,16,128]{2,1,0:T(8,128)(2,1)} %param.7) | copy-start | bytes 1572868
  4.2 25.5 %all-to-all-start = ((bf16[16,136,256]{2,1,0:T(8,128)(2,1)}), bf16[16,136,256]{2,1,0:T(8,128)(2,1)S(1)}, u32[]{:S(2)}, u32[]{:S(2)}) async-start(bf16[16,136,256]{2,1,0:T(8,128)(2,1)} %pad_maximum_fusion), calls=%async_computation | async-start | bytes 2228224 | tf_op jit(solution)/shard_map/all_to_all | solution.py:288
  39.9 3.1 %collective-permute-start = (f32[128,128]{1,0:T(8,128)S(1)}, f32[128,128]{1,0:T(8,128)S(1)}, u32[]{:S(2)}, u32[]{:S(2)}) collective-permute-start(f32[128,128]{1,0:T(8,128)S(1)} %get-tuple-element.26), channel_id=1, source_target_pairs={{0,16},{16,0},{1,17},{17,1},{2,18},{18,2},{3,19},{19,3},{4,20},{20... | collective-permute-start | bytes 196616 | tf_op jit(solution)/shard_map/ppermute | solution.py:317
  43.2 6.2 %collective-permute-start.2 = (f32[128,128]{1,0:T(8,128)S(1)}, f32[128,128]{1,0:T(8,128)S(1)}, u32[]{:S(2)}, u32[]{:S(2)}) collective-permute-start(f32[128,128]{1,0:T(8,128)S(1)} %shard_map.74.near_ref), channel_id=1, source_target_pairs={{0,32},{32,64},{64,96},{96,128},{128,160},{160,192},{192,224},{224... | collective-permute-start | bytes 196616 | tf_op jit(solution)/shard_map/ppermute | solution.py:322
  47.1 2.7 %collective-permute-start.1 = (f32[128,128]{1,0:T(8,128)S(1)}, f32[128,128]{1,0:T(8,128)S(1)}, u32[]{:S(2)}, u32[]{:S(2)}) collective-permute-start(f32[128,128]{1,0:T(8,128)S(1)} %shard_map.74.near_ref), channel_id=1, source_target_pairs={{0,16},{1,17},{2,18},{3,19},{4,20},{5,21},{6,22},{7,23},{8,24},{9,... | collective-permute-start | bytes 196616 | tf_op jit(solution)/shard_map/ppermute | solution.py:338
  49.9 8.4 %collective-permute-start.4 = (f32[128,128]{1,0:T(8,128)S(1)}, f32[128,128]{1,0:T(8,128)S(1)}, u32[]{:S(2)}, u32[]{:S(2)}) collective-permute-start(f32[128,128]{1,0:T(8,128)S(1)} %shard_map.75.near_ref), channel_id=1, source_target_pairs={{0,64},{32,96},{64,128},{96,160},{128,192},{160,224},{192,256},{22... | collective-permute-start | bytes 196616 | tf_op jit(solution)/shard_map/ppermute | solution.py:322
  56.3 2.9 %collective-permute-start.3 = (f32[128,128]{1,0:T(8,128)S(1)}, f32[128,128]{1,0:T(8,128)S(1)}, u32[]{:S(2)}, u32[]{:S(2)}) collective-permute-start(f32[128,128]{1,0:T(8,128)S(1)} %shard_map.75.near_ref), channel_id=1, source_target_pairs={{0,16},{1,17},{2,18},{3,19},{4,20},{5,21},{6,22},{7,23},{8,24},{9,... | collective-permute-start | bytes 196616 | tf_op jit(solution)/shard_map/ppermute | solution.py:338
  59.3 3.1 %collective-permute-start.5 = (f32[128,128]{1,0:T(8,128)S(1)}, f32[128,128]{1,0:T(8,128)S(1)}, u32[]{:S(2)}, u32[]{:S(2)}) collective-permute-start(f32[128,128]{1,0:T(8,128)S(1)} %shard_map.76.near_ref), channel_id=1, source_target_pairs={{0,16},{1,17},{2,18},{3,19},{4,20},{5,21},{6,22},{7,23},{8,24},{9,... | collective-permute-start | bytes 196616 | tf_op jit(solution)/shard_map/ppermute | solution.py:338
  62.5 22.7 %all-to-all-start.1 = ((bf16[16,128,256]{2,1,0:T(8,128)(2,1)}), bf16[16,128,256]{2,1,0:T(8,128)(2,1)S(1)}, u32[]{:S(2)}, u32[]{:S(2)}) async-start(bf16[16,128,256]{2,1,0:T(8,128)(2,1)} %pad_maximum_fusion.1), calls=%async_computation.1 | async-start | bytes 2097152 | tf_op jit(solution)/shard_map/all_to_all | solution.py:288
  66.1 11.2 %collective-permute-start.6 = (f32[128,128]{1,0:T(8,128)S(1)}, f32[128,128]{1,0:T(8,128)S(1)}, u32[]{:S(2)}, u32[]{:S(2)}) collective-permute-start(f32[128,128]{1,0:T(8,128)S(1)} %shard_map.76.near_ref), channel_id=1, source_target_pairs={{0,128},{32,160},{64,192},{96,224},{128,256},{160,288},{192,320},{... | collective-permute-start | bytes 196616 | tf_op jit(solution)/shard_map/ppermute | solution.py:322
  75.2 35.9 %collective-permute-start.11 = (f32[128,128]{1,0:T(8,128)S(1)}, f32[128,128]{1,0:T(8,128)S(1)}, u32[]{:S(2)}, u32[]{:S(2)}) collective-permute-start(f32[128,128]{1,0:T(8,128)S(1)} %get-tuple-element.24.map_ref), channel_id=1, source_target_pairs={{0,16},{1,17},{2,18},{3,19},{4,20},{5,21},{6,22},{7,23},{8,24},{9,... | collective-permute-start | bytes 196616 | tf_op jit(solution)/shard_map/ppermute | solution.py:318
  85.2 26.0 %collective-permute-start.10 = (f32[128,128]{1,0:T(8,128)S(1)}, f32[128,128]{1,0:T(8,128)S(1)}, u32[]{:S(2)}, u32[]{:S(2)}) collective-permute-start(f32[128,128]{1,0:T(8,128)S(1)} %shard_map.77), channel_id=1, source_target_pairs={{16,304},{48,336},{80,368},{112,400},{144,432},{176,464},{208,496}... | collective-permute-start | bytes 196616 | tf_op jit(solution)/shard_map/ppermute | solution.py:330
  85.9 25.4 %collective-permute-start.9 = (f32[128,128]{1,0:T(8,128)S(1)}, f32[128,128]{1,0:T(8,128)S(1)}, u32[]{:S(2)}, u32[]{:S(2)}) collective-permute-start(f32[128,128]{1,0:T(8,128)S(1)} %shard_map.77), channel_id=1, source_target_pairs={{16,288},{48,320},{80,352},{112,384},{144,416},{176,448},{208,480}... | collective-permute-start | bytes 196616 | tf_op jit(solution)/shard_map/ppermute | solution.py:330
  86.5 24.7 %collective-permute-start.8 = (f32[128,128]{1,0:T(8,128)S(1)}, f32[128,128]{1,0:T(8,128)S(1)}, u32[]{:S(2)}, u32[]{:S(2)}) collective-permute-start(f32[128,128]{1,0:T(8,128)S(1)} %shard_map.77), channel_id=1, source_target_pairs={{0,48},{16,32},{32,80},{48,64},{64,112},{80,96},{96,144},{112,128}... | collective-permute-start | bytes 196616 | tf_op jit(solution)/shard_map/ppermute | solution.py:330
  100.2 11.0 %collective-permute-start.7 = (f32[128,128]{1,0:T(8,128)S(1)}, f32[128,128]{1,0:T(8,128)S(1)}, u32[]{:S(2)}, u32[]{:S(2)}) collective-permute-start(f32[128,128]{1,0:T(8,128)S(1)} %shard_map.77), channel_id=1, source_target_pairs={{0,32},{32,64},{64,96},{96,128},{128,160},{160,192},{192,224},{224... | collective-permute-start | bytes 196616 | tf_op jit(solution)/shard_map/ppermute | solution.py:322
  104.2 7.1 %copy-start = (f32[128]{0:T(128)S(1)}, f32[128]{0:T(128)}, u32[]{:S(2)}) copy-start(f32[128]{0:T(128)} %param.13) | copy-start | bytes 1540
where the time goes:
time: 114 us; the launch traced here: 113 us
  starting transfers between devices  58.9 us (52%)
  waiting for transfers between devices  28.7 us (25%)
  Pallas kernels  19.7 us (17%)
  other arithmetic  3.75 us (3%)
  local copies, waits for them, and re-layouts  1.81 us (2%)
    all_to_all x2, waiting for transfers between devices, to_heads(): lax.all_to_all(array, 'head', split_axis=0, concat_axis=0, tiled=True)  24.8 us
    ppermute x4, starting transfers between devices, up(): return lax.ppermute(x, 'z', [(i, i + d) for i in range(z - d)])  23.3 us
    pallas_call x7, Pallas kernels, call(): pl.pallas_call(kernel, out_shape=[*out_shape, *(pltpu.HBM(o.shape, o.dtyp...  19.7 us
    ppermute x3, starting transfers between devices, cross(): return lax.ppermute(x, ('z', 'c'), pairs)  15 us
    all_to_all x2, starting transfers between devices, to_heads(): lax.all_to_all(array, 'head', split_axis=0, concat_axis=0, tiled=True)  10.7 us
    ppermute x3, starting transfers between devices, layer(): maps = lax.ppermute(window, 'c', [(0, 1)])  6.02 us
  transfers between devices with their start and end apart: 14, of which 8 were waited for; matrix products, arithmetic and copies ran while one was open for 1% of the time, Pallas kernels for 6%

commit v1 on v0

--- a/solution.py
+++ b/solution.py
@@ -172,8 +172,16 @@
     ]
     for copy in copies:
         copy.start()
-    node_ref, en_ref, grow_ref, wu_hi_ref, wu_lo_ref = buffers
+    en_ref, wu_hi_ref, wu_lo_ref, grow_ref, node_ref = buffers
     copies[0].wait()
+    mixing = [
+        split2(en_ref[b] * dot_nt(q_ref[b, :, :N], kv_ref[b, :N, :N])) for b in range(blocks)
+    ]
+    copies[1].wait()
+    copies[2].wait()
+    mixed = [wide_mm(mixing[b], wu_hi_ref[b], wu_lo_ref[b]) for b in range(blocks)]
+    copies[3].wait()
+    copies[4].wait()
     carried = {}
     base, width = {1: 0}, 1
     while width * 2 < blocks:
@@ -185,16 +193,12 @@
             node = node_ref[base[step] + (b - step) // step]
             carried[b] = compose(node, carried[b - step]) if b > step else node
         step //= 2
-    for copy in copies[1:]:
-        copy.wait()
     for b in range(blocks):
         q = q_ref[b, :, :N]
-        mixing = en_ref[b] * dot_nt(q, kv_ref[b, :N, :N])
-        mixed = wide_mm(split2(mixing), wu_hi_ref[b], wu_lo_ref[b])
         q32 = q.astype(F32)
         scale = lax.rsqrt(jnp.sum(q32 * q32, axis=1, keepdims=True) + EPS) * N**-0.5
-        reach = grow_ref[b] * q32 - mixed[:, :N]
-        local = mixed[:, N:]
+        reach = grow_ref[b] * q32 - mixed[b][:, :N]
+        local = mixed[b][:, N:]
         if b:
             high, low = split2(carried[b])
             out = wide_mm(split2(reach), high, low)
@@ -315,7 +319,6 @@
     )
     swap = [(0, 1), (1, 0)]
     got = lax.ppermute(send, "c", swap)
-    first_map = lax.ppermute(own_map, "c", [(0, 1)])
     chip = call(pair_kernel, [square], near(own_map, own_off, got), core)[0]
 
     def up(x, d):
@@ -341,17 +344,18 @@
             qg = to_heads(qg)
         window = join(window, maps, far)
         span *= 2
-    qg, window = lax.optimization_barrier((qg, window))
     far0 = cross(window, span + 1, 1, 0)
     far1 = cross(window, span + 1, 1, 1)
     own = up(window, 1)
     other = cross(window, 1, 0, 1, 1, 0)
+    own_map, own = lax.optimization_barrier((own_map, own))
+    first_map = lax.ppermute(own_map, "c", [(0, 1)])
     half = kept(blocks, N, N, dtype=BF16)
     r0, r1_hi, r1_lo = call(
         reach_kernel,
         [kept(blocks, N, N), half, half],
         near(kv, qg),
-        remote=[nodes, en, grow, wu_hi, wu_lo],
+        remote=[en, wu_hi, wu_lo, grow, nodes],
         sems=5,
     )
     (out,) = call(

time: 114 us -> 109 us (0.956)
  the two profiles are of different devices: /device:TPU:32 before, /device:TPU:34 now
where the time goes in v1:
time: 109 us
  starting transfers between devices  64.3 us (59%)
  waiting for transfers between devices  20.9 us (19%)
  Pallas kernels  17.4 us (16%)
  other arithmetic  3.75 us (3%)
  local copies, waits for them, and re-layouts  1.81 us (2%)
    ppermute x4, starting transfers between devices, up(): return lax.ppermute(x, 'z', [(i, i + d) for i in range(z - d)])  24.1 us
    ppermute x3, starting transfers between devices, cross(): return lax.ppermute(x, ('z', 'c'), pairs)  17.8 us
    pallas_call x7, Pallas kernels, call(): pl.pallas_call(kernel, out_shape=[*out_shape, *(pltpu.HBM(o.shape, o.dtyp...  17.4 us
    all_to_all x2, waiting for transfers between devices, to_heads(): lax.all_to_all(array, 'head', split_axis=0, concat_axis=0, tiled=True)  15.1 us
    all_to_all x2, starting transfers between devices, to_heads(): lax.all_to_all(array, 'head', split_axis=0, concat_axis=0, tiled=True)  13 us
    ppermute x3, starting transfers between devices, layer(): maps = lax.ppermute(window, 'c', [(0, 1)])  6.02 us
    ppermute x4, waiting for transfers between devices, up(): return lax.ppermute(x, 'z', [(i, i + d) for i in range(z - d)])  2.51 us
  transfers between devices with their start and end apart: 14, of which 7 were waited for; matrix products, arithmetic and copies ran while one was open for 1% of the time, Pallas kernels for 4%

profile of v1, /device:TPU:34, one launch (start us, length us, event | category | flops | bytes accessed | tf_op | source)
XLA Modules:
  0.0 108.5 jit_solution(10117851023233883144)
XLA Ops:
  0.7 0.7 fusion.15
  1.5 1.5 %copy_bitcast_fusion.2 = (bf16[16,128,128]{2,1,0:T(8,128)(2,1)S(1)}, bf16[16,128,128]{2,1,0:T(8,128)(2,1)S(1)}) fusion(bf16[128,16,128]{2,1,0:T(8,128)(2,1)} %param.9, bf16[128,16,128]{2,1,0:T(8,128)(2,1)} %param.8), kind=kLoop, calls=%fused_computation.4 | loop fusion | bytes 2097152 | tf_op jit(solution)/shard_map/transpose | solution.py:288
  3.1 1.2 %pad_maximum_fusion = bf16[16,136,256]{2,1,0:T(8,128)(2,1)} fusion(bf16[16,8,256]{2,1,0:T(8,128)(2,1)S(1)} %fusion.8, bf16[16,128,128]{2,1,0:T(8,128)(2,1)S(1)} %get-tuple-element.45, bf16[16,128,128]{2,1,0:T(8,128)(2,1)S(1)} %get-tuple-element.46), kind=kLoop, calls=%fused_computation | loop fusion | flops 3342336 | bytes 2228224 | tf_op jit(solution)/shard_map/concatenate | solution.py:304
  4.2 7.5 %all-to-all-start = ((bf16[16,136,256]{2,1,0:T(8,128)(2,1)}), bf16[16,136,256]{2,1,0:T(8,128)(2,1)S(1)}, u32[]{:S(2)}, u32[]{:S(2)}) async-start(bf16[16,136,256]{2,1,0:T(8,128)(2,1)} %pad_maximum_fusion), calls=%async_computation | async-start | bytes 2228224 | tf_op jit(solution)/shard_map/all_to_all | solution.py:292
  12.0 1.1 %pad_maximum_fusion.1 = bf16[16,128,256]{2,1,0:T(8,128)(2,1)} fusion(bf16[16,128,128]{2,1,0:T(8,128)(2,1)S(1)} %get-tuple-element.47, bf16[16,128,128]{2,1,0:T(8,128)(2,1)S(1)} %get-tuple-element.48), kind=kLoop, calls=%fused_computation.1 | loop fusion | flops 2097152 | bytes 2097152 | tf_op jit(solution)/shard_map/concatenate | solution.py:305
  13.1 15.1 %all-to-all-done.kv_ref = bf16[16,136,256]{2,1,0:T(8,128)(2,1)S(1)} async-done(((bf16[16,136,256]{2,1,0:T(8,128)(2,1)}), bf16[16,136,256]{2,1,0:T(8,128)(2,1)S(1)}, u32[]{:S(2)}, u32[]{:S(2)}) %all-to-all-start) | async-done | bytes 1114144 | tf_op jit(solution)/shard_map/all_to_all | solution.py:292
  28.2 10.1 %shard_map.73 = (f32[128,128]{1,0:T(8,128)S(1)}, f32[128,128]{1,0:T(8,128)S(1)}, f32[128,128]{1,0:T(8,128)S(1)}, f32[16,128,128]{2,1,0:T(8,128)}, f32[16,128,128...) custom-call(s32[1]{0:T(128)} %bitcast.core_ref, ...), custom_call_target="tpu_custom_call" | custom-call | tf_op jit(solution)/shard_map/pallas_call | solution.py:257
  38.4 1.9 %collective-permute-start = (f32[128,128]{1,0:T(8,128)S(1)}, f32[128,128]{1,0:T(8,128)S(1)}, u32[]{:S(2)}, u32[]{:S(2)}) collective-permute-start(f32[128,128]{1,0:T(8,128)S(1)} %get-tuple-element.26), channel_id=1, source_target_pairs={{0,16},{16,0},{1,17},{17,1},{2,18},{18,2},{3,19},{19,3},{4,20},{20... | collective-permute-start | bytes 196616 | tf_op jit(solution)/shard_map/ppermute | solution.py:321
  40.3 1.2 %collective-permute-done.got_ref.off_ref = f32[128,128]{1,0:T(8,128)S(1)} collective-permute-done((f32[128,128]{1,0:T(8,128)S(1)}, f32[128,128]{1,0:T(8,128)S(1)}, u32[]{:S(2)}, u32[]{:S(2)}) %collective-permute-start) | collective-permute-done | bytes 65568 | tf_op jit(solution)/shard_map/ppermute | solution.py:321
  41.7 3.8 %collective-permute-start.2 = (f32[128,128]{1,0:T(8,128)S(1)}, f32[128,128]{1,0:T(8,128)S(1)}, u32[]{:S(2)}, u32[]{:S(2)}) collective-permute-start(f32[128,128]{1,0:T(8,128)S(1)} %shard_map.74.near_ref), channel_id=1, source_target_pairs={{0,32},{32,64},{64,96},{96,128},{128,160},{160,192},{192,224},{224... | collective-permute-start | bytes 196616 | tf_op jit(solution)/shard_map/ppermute | solution.py:325
  45.5 1.8 %collective-permute-start.1 = (f32[128,128]{1,0:T(8,128)S(1)}, f32[128,128]{1,0:T(8,128)S(1)}, u32[]{:S(2)}, u32[]{:S(2)}) collective-permute-start(f32[128,128]{1,0:T(8,128)S(1)} %shard_map.74.near_ref), channel_id=1, source_target_pairs={{0,16},{1,17},{2,18},{3,19},{4,20},{5,21},{6,22},{7,23},{8,24},{9,... | collective-permute-start | bytes 196616 | tf_op jit(solution)/shard_map/ppermute | solution.py:341
  48.4 6.4 %collective-permute-start.4 = (f32[128,128]{1,0:T(8,128)S(1)}, f32[128,128]{1,0:T(8,128)S(1)}, u32[]{:S(2)}, u32[]{:S(2)}) collective-permute-start(f32[128,128]{1,0:T(8,128)S(1)} %shard_map.75.near_ref), channel_id=1, source_target_pairs={{0,64},{32,96},{64,128},{96,160},{128,192},{160,224},{192,256},{22... | collective-permute-start | bytes 196616 | tf_op jit(solution)/shard_map/ppermute | solution.py:325
  54.8 2.0 %collective-permute-start.3 = (f32[128,128]{1,0:T(8,128)S(1)}, f32[128,128]{1,0:T(8,128)S(1)}, u32[]{:S(2)}, u32[]{:S(2)}) collective-permute-start(f32[128,128]{1,0:T(8,128)S(1)} %shard_map.75.near_ref), channel_id=1, source_target_pairs={{0,16},{1,17},{2,18},{3,19},{4,20},{5,21},{6,22},{7,23},{8,24},{9,... | collective-permute-start | bytes 196616 | tf_op jit(solution)/shard_map/ppermute | solution.py:341
  56.8 0.9 collective-permute-done.3.map_ref
  57.8 2.3 %collective-permute-start.5 = (f32[128,128]{1,0:T(8,128)S(1)}, f32[128,128]{1,0:T(8,128)S(1)}, u32[]{:S(2)}, u32[]{:S(2)}) collective-permute-start(f32[128,128]{1,0:T(8,128)S(1)} %shard_map.76.near_ref), channel_id=1, source_target_pairs={{0,16},{1,17},{2,18},{3,19},{4,20},{5,21},{6,22},{7,23},{8,24},{9,... | collective-permute-start | bytes 196616 | tf_op jit(solution)/shard_map/ppermute | solution.py:341
  60.1 0.9 collective-permute-done.5.map_ref
  60.9 5.5 %all-to-all-start.1 = ((bf16[16,128,256]{2,1,0:T(8,128)(2,1)}), bf16[16,128,256]{2,1,0:T(8,128)(2,1)S(1)}, u32[]{:S(2)}, u32[]{:S(2)}) async-start(bf16[16,128,256]{2,1,0:T(8,128)(2,1)} %pad_maximum_fusion.1), calls=%async_computation.1 | async-start | bytes 2097152 | tf_op jit(solution)/shard_map/all_to_all | solution.py:292
  66.5 9.1 %collective-permute-start.6 = (f32[128,128]{1,0:T(8,128)S(1)}, f32[128,128]{1,0:T(8,128)S(1)}, u32[]{:S(2)}, u32[]{:S(2)}) collective-permute-start(f32[128,128]{1,0:T(8,128)S(1)} %shard_map.76.near_ref), channel_id=1, source_target_pairs={{0,128},{32,160},{64,192},{96,224},{128,256},{160,288},{192,320},{... | collective-permute-start | bytes 196616 | tf_op jit(solution)/shard_map/ppermute | solution.py:325
  75.6 2.0 %collective-permute-done.6.far_ref = f32[128,128]{1,0:T(8,128)S(1)} collective-permute-done((f32[128,128]{1,0:T(8,128)S(1)}, f32[128,128]{1,0:T(8,128)S(1)}, u32[]{:S(2)}, u32[]{:S(2)}) %collective-permute-start.6) | collective-permute-done | bytes 65568 | tf_op jit(solution)/shard_map/ppermute | solution.py:325
  77.7 4.8 %collective-permute-start.7 = (f32[128,128]{1,0:T(8,128)S(1)}, f32[128,128]{1,0:T(8,128)S(1)}, u32[]{:S(2)}, u32[]{:S(2)}) collective-permute-start(f32[128,128]{1,0:T(8,128)S(1)} %shard_map.78), channel_id=1, source_target_pairs={{0,32},{32,64},{64,96},{96,128},{128,160},{160,192},{192,224},{224... | collective-permute-start | bytes 196616 | tf_op jit(solution)/shard_map/ppermute | solution.py:325
  83.9 16.4 %collective-permute-start.8 = (f32[128,128]{1,0:T(8,128)S(1)}, f32[128,128]{1,0:T(8,128)S(1)}, u32[]{:S(2)}, u32[]{:S(2)}) collective-permute-start(f32[128,128]{1,0:T(8,128)S(1)} %shard_map.78), channel_id=1, source_target_pairs={{0,48},{16,32},{32,80},{48,64},{64,112},{80,96},{96,144},{112,128}... | collective-permute-start | bytes 196616 | tf_op jit(solution)/shard_map/ppermute | solution.py:333
  100.3 1.5 %collective-permute-start.11 = (f32[128,128]{1,0:T(8,128)S(1)}, f32[128,128]{1,0:T(8,128)S(1)}, u32[]{:S(2)}, u32[]{:S(2)}) collective-permute-start(f32[128,128]{1,0:T(8,128)S(1)} %get-tuple-element.38.map_ref), channel_id=1, source_target_pairs={{0,16},{1,17},{2,18},{3,19},{4,20},{5,21},{6,22},{7,23},{8,24},{9,... | collective-permute-start | bytes 196616 | tf_op jit(solution)/shard_map/ppermute | solution.py:352
  101.8 4.7 %shard_map.77 = (f32[16,128,128]{2,1,0:T(8,128)S(1)}, bf16[16,128,128]{2,1,0:T(8,128)(2,1)S(1)}, bf16[16,128,128]{2,1,0:T(8,128)(2,1)S(1)}) custom-call(bf16[16,136,256]{2,1,0:T(8,128)(2,1)S(1)} %all-to-all-done.kv_ref, bf16[16,128,256]{2,1,0:T(8,128)(2,1)S(1)} %all-to-all-done.1.q_ref.gate_ref, f32[16,128,128]{2,1,0:T(8,128)} %get-tuple-element.28.rest_0_, ...), custom_call_target="tpu_custom_call" | custom-call | tf_op jit(solution)/shard_map/pallas_call | solution.py:257
  106.6 1.9 %shard_map.79 = bf16[16,128,128]{2,1,0:T(8,128)(2,1)} custom-call(s32[1]{0:T(128)} %bitcast.core_ref, f32[16,128,128]{2,1,0:T(8,128)S(1)} %get-tuple-element.33.r0_ref, bf16[16,128,128]{2,1,0:T(8,128)(2,1)S(1)} %get-tuple-element.34.hi_ref, bf16[16,128,128]{2,1,0:T(8,128)(2,1)S(1)} %get-tuple-element.35.lo_ref, ...), custom_call_target="tpu_custom_call" | custom-call | tf_op jit(solution)/shard_map/pallas_call | solution.py:257
  (30 shorter events, 4.0 us)
Async XLA Ops:
  3.1 8.7 %copy-start.1 = (bf16[128,16,128]{2,1,0:T(8,128)(2,1)S(1)}, bf16[128,16,128]{2,1,0:T(8,128)(2,1)}, u32[]{:S(2)}) copy-start(bf16[128,16,128]{2,1,0:T(8,128)(2,1)} %param.12) | copy-start | bytes 1572868
  3.1 8.7 %copy-start.2 = (bf16[128,16,128]{2,1,0:T(8,128)(2,1)S(1)}, bf16[128,16,128]{2,1,0:T(8,128)(2,1)}, u32[]{:S(2)}) copy-start(bf16[128,16,128]{2,1,0:T(8,128)(2,1)} %param.7) | copy-start | bytes 1572868
  4.2 24.0 %all-to-all-start = ((bf16[16,136,256]{2,1,0:T(8,128)(2,1)}), bf16[16,136,256]{2,1,0:T(8,128)(2,1)S(1)}, u32[]{:S(2)}, u32[]{:S(2)}) async-start(bf16[16,136,256]{2,1,0:T(8,128)(2,1)} %pad_maximum_fusion), calls=%async_computation | async-start | bytes 2228224 | tf_op jit(solution)/shard_map/all_to_all | solution.py:292
  38.4 3.1 %collective-permute-start = (f32[128,128]{1,0:T(8,128)S(1)}, f32[128,128]{1,0:T(8,128)S(1)}, u32[]{:S(2)}, u32[]{:S(2)}) collective-permute-start(f32[128,128]{1,0:T(8,128)S(1)} %get-tuple-element.26), channel_id=1, source_target_pairs={{0,16},{16,0},{1,17},{17,1},{2,18},{18,2},{3,19},{19,3},{4,20},{20... | collective-permute-start | bytes 196616 | tf_op jit(solution)/shard_map/ppermute | solution.py:321
  41.7 6.2 %collective-permute-start.2 = (f32[128,128]{1,0:T(8,128)S(1)}, f32[128,128]{1,0:T(8,128)S(1)}, u32[]{:S(2)}, u32[]{:S(2)}) collective-permute-start(f32[128,128]{1,0:T(8,128)S(1)} %shard_map.74.near_ref), channel_id=1, source_target_pairs={{0,32},{32,64},{64,96},{96,128},{128,160},{160,192},{192,224},{224... | collective-permute-start | bytes 196616 | tf_op jit(solution)/shard_map/ppermute | solution.py:325
  45.5 2.7 %collective-permute-start.1 = (f32[128,128]{1,0:T(8,128)S(1)}, f32[128,128]{1,0:T(8,128)S(1)}, u32[]{:S(2)}, u32[]{:S(2)}) collective-permute-start(f32[128,128]{1,0:T(8,128)S(1)} %shard_map.74.near_ref), channel_id=1, source_target_pairs={{0,16},{1,17},{2,18},{3,19},{4,20},{5,21},{6,22},{7,23},{8,24},{9,... | collective-permute-start | bytes 196616 | tf_op jit(solution)/shard_map/ppermute | solution.py:341
  48.4 8.4 %collective-permute-start.4 = (f32[128,128]{1,0:T(8,128)S(1)}, f32[128,128]{1,0:T(8,128)S(1)}, u32[]{:S(2)}, u32[]{:S(2)}) collective-permute-start(f32[128,128]{1,0:T(8,128)S(1)} %shard_map.75.near_ref), channel_id=1, source_target_pairs={{0,64},{32,96},{64,128},{96,160},{128,192},{160,224},{192,256},{22... | collective-permute-start | bytes 196616 | tf_op jit(solution)/shard_map/ppermute | solution.py:325
  54.8 2.9 %collective-permute-start.3 = (f32[128,128]{1,0:T(8,128)S(1)}, f32[128,128]{1,0:T(8,128)S(1)}, u32[]{:S(2)}, u32[]{:S(2)}) collective-permute-start(f32[128,128]{1,0:T(8,128)S(1)} %shard_map.75.near_ref), channel_id=1, source_target_pairs={{0,16},{1,17},{2,18},{3,19},{4,20},{5,21},{6,22},{7,23},{8,24},{9,... | collective-permute-start | bytes 196616 | tf_op jit(solution)/shard_map/ppermute | solution.py:341
  57.8 3.1 %collective-permute-start.5 = (f32[128,128]{1,0:T(8,128)S(1)}, f32[128,128]{1,0:T(8,128)S(1)}, u32[]{:S(2)}, u32[]{:S(2)}) collective-permute-start(f32[128,128]{1,0:T(8,128)S(1)} %shard_map.76.near_ref), channel_id=1, source_target_pairs={{0,16},{1,17},{2,18},{3,19},{4,20},{5,21},{6,22},{7,23},{8,24},{9,... | collective-permute-start | bytes 196616 | tf_op jit(solution)/shard_map/ppermute | solution.py:341
  60.9 40.9 %all-to-all-start.1 = ((bf16[16,128,256]{2,1,0:T(8,128)(2,1)}), bf16[16,128,256]{2,1,0:T(8,128)(2,1)S(1)}, u32[]{:S(2)}, u32[]{:S(2)}) async-start(bf16[16,128,256]{2,1,0:T(8,128)(2,1)} %pad_maximum_fusion.1), calls=%async_computation.1 | async-start | bytes 2097152 | tf_op jit(solution)/shard_map/all_to_all | solution.py:292
  66.5 11.1 %collective-permute-start.6 = (f32[128,128]{1,0:T(8,128)S(1)}, f32[128,128]{1,0:T(8,128)S(1)}, u32[]{:S(2)}, u32[]{:S(2)}) collective-permute-start(f32[128,128]{1,0:T(8,128)S(1)} %shard_map.76.near_ref), channel_id=1, source_target_pairs={{0,128},{32,160},{64,192},{96,224},{128,256},{160,288},{192,320},{... | collective-permute-start | bytes 196616 | tf_op jit(solution)/shard_map/ppermute | solution.py:325
  77.7 22.6 %collective-permute-start.7 = (f32[128,128]{1,0:T(8,128)S(1)}, f32[128,128]{1,0:T(8,128)S(1)}, u32[]{:S(2)}, u32[]{:S(2)}) collective-permute-start(f32[128,128]{1,0:T(8,128)S(1)} %shard_map.78), channel_id=1, source_target_pairs={{0,32},{32,64},{64,96},{96,128},{128,160},{160,192},{192,224},{224... | collective-permute-start | bytes 196616 | tf_op jit(solution)/shard_map/ppermute | solution.py:325
  82.5 24.0 %collective-permute-start.10 = (f32[128,128]{1,0:T(8,128)S(1)}, f32[128,128]{1,0:T(8,128)S(1)}, u32[]{:S(2)}, u32[]{:S(2)}) collective-permute-start(f32[128,128]{1,0:T(8,128)S(1)} %shard_map.78), channel_id=1, source_target_pairs={{16,304},{48,336},{80,368},{112,400},{144,432},{176,464},{208,496}... | collective-permute-start | bytes 196616 | tf_op jit(solution)/shard_map/ppermute | solution.py:333
  83.2 23.4 %collective-permute-start.9 = (f32[128,128]{1,0:T(8,128)S(1)}, f32[128,128]{1,0:T(8,128)S(1)}, u32[]{:S(2)}, u32[]{:S(2)}) collective-permute-start(f32[128,128]{1,0:T(8,128)S(1)} %shard_map.78), channel_id=1, source_target_pairs={{16,288},{48,320},{80,352},{112,384},{144,416},{176,448},{208,480}... | collective-permute-start | bytes 196616 | tf_op jit(solution)/shard_map/ppermute | solution.py:333
  83.9 22.7 %collective-permute-start.8 = (f32[128,128]{1,0:T(8,128)S(1)}, f32[128,128]{1,0:T(8,128)S(1)}, u32[]{:S(2)}, u32[]{:S(2)}) collective-permute-start(f32[128,128]{1,0:T(8,128)S(1)} %shard_map.78), channel_id=1, source_target_pairs={{0,48},{16,32},{32,80},{48,64},{64,112},{80,96},{96,144},{112,128}... | collective-permute-start | bytes 196616 | tf_op jit(solution)/shard_map/ppermute | solution.py:333
  100.3 6.3 %collective-permute-start.11 = (f32[128,128]{1,0:T(8,128)S(1)}, f32[128,128]{1,0:T(8,128)S(1)}, u32[]{:S(2)}, u32[]{:S(2)}) collective-permute-start(f32[128,128]{1,0:T(8,128)S(1)} %get-tuple-element.38.map_ref), channel_id=1, source_target_pairs={{0,16},{1,17},{2,18},{3,19},{4,20},{5,21},{6,22},{7,23},{8,24},{9,... | collective-permute-start | bytes 196616 | tf_op jit(solution)/shard_map/ppermute | solution.py:352
  101.8 4.8 %copy-start = (f32[128]{0:T(128)S(1)}, f32[128]{0:T(128)}, u32[]{:S(2)}) copy-start(f32[128]{0:T(128)} %param.13) | copy-start | bytes 1540

commit v2 on v1

v2 whole, which is shorter than its diff:
```python
import jax
import jax.numpy as jnp
from jax import lax
from jax.experimental import pallas as pl
from jax.experimental.pallas import tpu as pltpu
from jax.sharding import Mesh
from jax.sharding import PartitionSpec as P


F32 = jnp.float32
BF16 = jnp.bfloat16
N = 128
EPS = 1e-06
SUB = 16


def dot(a, b):
    return jnp.dot(a, b, preferred_element_type=F32)


def dot_nt(a, b):
    return lax.dot_general(a, b, (((1,), (1,)), ((), ())), preferred_element_type=F32)


def split2(x):
    high = x.astype(BF16)
    return high, (x - high.astype(F32)).astype(BF16)


def lanes(*parts):
    return jnp.concatenate(parts, axis=1)


def rows(*parts):
    return jnp.concatenate(parts, axis=0)


def square_mm(a_parts, b_parts):
    b_both = lanes(*b_parts)
    both = dot(lanes(*a_parts), rows(b_both, b_both))
    return both[:, :N] + both[:, N:]


def wide_mm(a_parts, b_high, b_low):
    return dot(lanes(*a_parts), rows(b_high, b_high)) + dot(a_parts[0], b_low)


def compose(later, earlier):
    high, low = split2(earlier)
    out = wide_mm(split2(later[:, :N]), high, low)
    return out + lanes(jnp.zeros((N, N), F32), later[:, N:])


def iotas():
    return lax.broadcasted_iota(jnp.int32, (N, N), 0), lax.broadcasted_iota(jnp.int32, (N, N), 1)


def pack_kernel(k_ref, v_ref, beta_ref, decay_ref, out_ref):
    heads, tokens = out_ref.shape[0], k_ref.shape[0] // out_ref.shape[0]
    span = N * 2 // heads
    shape2 = (2 * N, 2 * N)
    r = lax.broadcasted_iota(jnp.int32, shape2, 0)
    c = lax.broadcasted_iota(jnp.int32, shape2, 1)
    order = (c == r % span * heads + r // span).astype(F32).astype(BF16)
    for i in range(tokens // span):
        part = pl.ds(2 * N * i, 2 * N)
        moved = dot(order, lanes(k_ref[part, :], v_ref[part, :])).astype(BF16)
        for h in range(heads):
            out_ref[h, span * i : span * (i + 1), :] = moved[span * h : span * (h + 1), :]
    both = lanes(decay_ref[...].T, beta_ref[...].T)
    high = both.astype(BF16).astype(F32)
    low = both - high
    row = lax.broadcasted_iota(jnp.int32, (8, 2 * N), 0)
    for h in range(heads):
        aux = jnp.where(row == 0, high[h : h + 1, :], jnp.where(row == 1, low[h : h + 1, :], 0.0))
        out_ref[h, tokens : tokens + 8, :] = aux.astype(BF16)


def terms_kernel(kv_ref, total_ref, *rest):
    outs, (en_ref, wu_hi_ref, wu_lo_ref, grow_ref, node_ref), sems = rest[:5], rest[5:10], rest[10]
    blocks = kv_ref.shape[0]
    copies = []

    def save(which, first=0, count=blocks):
        part = pl.ds(first, count)
        copies.append(
            pltpu.make_async_copy(rest[5 + which].at[part], outs[which].at[part], sems.at[len(copies)])
        )
        copies[-1].start()

    r, c = iotas()
    one = lambda cond: cond.astype(F32).astype(BF16)
    lower = one(r >= c)
    eye = (r == c).astype(F32)
    inclusive = r >= c
    strict = r > c
    picks = lanes(one(strict), jnp.ones((N, N), BF16))
    picks = rows(picks, picks)
    lane16 = lax.broadcasted_iota(jnp.int32, (SUB, N), 1)
    row16 = lax.broadcasted_iota(jnp.int32, (SUB, N), 0)
    start16 = (row16 == lane16 % SUB).astype(F32)
    base16 = lane16 // SUB * SUB
    merge_masks = [one((r // m == c // m + 1) & (c // m % 2 == 0)) for m in (16, 32, 64)]
    group = range(blocks)

    keys = [kv_ref[b, :N, :N] for b in group]
    kk = [dot_nt(k, k) for k in keys]
    aux = [kv_ref[b, N : N + 8, :] for b in group]
    summed = [dot(lanes(lower * a[0:1, :N], lower * a[1:2, :N]), picks) for a in aux]
    cum = [s[:, N:] for s in summed]
    beta_row = []
    grow_row = []
    nk_row = []
    nk_col = []
    low = []
    for b in group:
        a = aux[b].astype(F32)
        beta_row.append(a[0:1, N:] + a[1:2, N:])
        grow_row.append(jnp.exp(jnp.sum(eye * cum[b], axis=0, keepdims=True)))
        diag = eye * kk[b]
        nk_row.append(lax.rsqrt(jnp.sum(diag, axis=0, keepdims=True) + EPS))
        nk_col.append(lax.rsqrt(jnp.sum(diag, axis=1, keepdims=True) + EPS))
        beta_col = jnp.sum(eye * beta_row[b], axis=1, keepdims=True)
        fade_n = jnp.exp(summed[b][:, :N]) * nk_row[b]
        en_ref[b] = jnp.where(inclusive, fade_n, 0.0)
        low.append(jnp.where(strict, fade_n * (kk[b] * (beta_col * nk_col[b])), 0.0))
        grow_ref[b] = jnp.broadcast_to(grow_row[b], (8, N))
    save(0)
    save(3)
    inv = []
    for b in group:
        small = sum(
            jnp.where(lane16 // SUB == s, low[b][SUB * s : SUB * (s + 1)], 0.0) for s in range(N // SUB)
        )
        x = start16
        for j in range(SUB - 1):
            col = jnp.take_along_axis(small, base16 + j, axis=1)
            x = x - col * x[j : j + 1, :]
        inv.append(rows(*[jnp.where(lane16 // SUB == s, x, 0.0) for s in range(N // SUB)]))
    low_parts = [split2(x) for x in low]
    for mask in merge_masks:
        parts = [split2(x) for x in inv]
        left = [square_mm(parts[b], [p * mask for p in low_parts[b]]) for b in group]
        left = [split2(x) for x in left]
        inv = [inv[b] - square_mm(left[b], parts[b]) for b in group]
    for_u = [inv[b] * beta_row[b] for b in group]
    for_w = [split2(for_u[b] * (grow_row[b] * nk_row[b])) for b in group]
    for_u = [split2(x) for x in for_u]
    w = [dot(lanes(*for_w[b]), rows(keys[b], keys[b])) for b in group]
    values = [kv_ref[b, :N, N:] for b in group]
    u = [dot(lanes(*for_u[b]), rows(values[b], values[b])) for b in group]
    wu = [lanes(w[b], u[b]) for b in group]
    for b in group:
        wu_hi_ref[b], wu_lo_ref[b] = split2(wu[b])
    save(1)
    save(2)
    last = [x[N - 1 : N, :] for x in cum]
    tail = [jnp.exp(last[b] - cum[b]) * nk_col[b] for b in group]
    faded = [split2(wu[b] * lanes(tail[b], tail[b])) for b in group]
    key_t = [k.T for k in keys]
    out = [dot(lanes(key_t[b], key_t[b]), rows(*faded[b])) for b in group]
    pairs = [lanes(eye * jnp.exp(last[b]) - out[b][:, :N], out[b][:, N:]) for b in group]
    spot = 0
    while len(pairs) > 1:
        for i in range(0, len(pairs), 2):
            node_ref[spot + i // 2] = pairs[i]
        save(4, spot, len(pairs) // 2)
        spot += len(pairs) // 2
        pairs = [compose(pairs[i + 1], pairs[i]) for i in range(0, len(pairs), 2)]
    total_ref[...] = pairs[0]
    for copy in copies:
        copy.wait()


def reach_kernel(kv_ref, qg_ref, gain_ref, *rest):
    sources, (r0_ref, hi_ref, lo_ref, gate_ref) = rest[:5], rest[5:9]
    buffers, sems = rest[9:14], rest[14]
    blocks = kv_ref.shape[0]
    copies = [
        pltpu.make_async_copy(sources[i], buffers[i], sems.at[i]) for i in range(len(sources))
    ]
    for copy in copies:
        copy.start()
    en_ref, wu_hi_ref, wu_lo_ref, grow_ref, node_ref = buffers
    r, c = iotas()
    eye = (r == c).astype(F32)
    for b in range(blocks):
        gate = qg_ref[b, :, N:].astype(F32)
        gate_ref[b] = gate / (1.0 + jnp.exp(-gate)) * gain_ref[...]
    copies[0].wait()
    mixing = [
        split2(en_ref[b] * dot_nt(qg_ref[b, :, :N], kv_ref[b, :N, :N])) for b in range(blocks)
    ]
    copies[1].wait()
    copies[2].wait()
    mixed = [wide_mm(mixing[b], wu_hi_ref[b], wu_lo_ref[b]) for b in range(blocks)]
    copies[3].wait()
    copies[4].wait()
    carried = {}
    base, width = {1: 0}, 1
    while width * 2 < blocks:
        base[width * 2] = base[width] + blocks // width // 2
        width *= 2
    step = blocks // 2
    while step:
        for b in range(step, blocks, 2 * step):
            node = node_ref[base[step] + (b - step) // step // 2]
            carried[b] = compose(node, carried[b - step]) if b > step else node
        step //= 2
    for b in range(blocks):
        q32 = qg_ref[b, :, :N].astype(F32)
        scale = lax.rsqrt(jnp.sum(q32 * q32, axis=1, keepdims=True) + EPS) * N**-0.5
        grow_col = jnp.sum(eye * grow_ref[b, 0:1, :], axis=1, keepdims=True)
        reach = grow_col * q32 - mixed[b][:, :N]
        local = mixed[b][:, N:]
        if b:
            high, low = split2(carried[b])
            out = wide_mm(split2(reach), high, low)
            reach, local = out[:, :N], local + out[:, N:]
        r0_ref[b] = local * scale
        hi_ref[b], lo_ref[b] = split2(reach * scale)


def advance(left, right, extra):
    return square_mm(split2(left), split2(right)) + extra


def pair_kernel(core_ref, own_ref, got_ref, out_ref):
    first = core_ref[0] == 0
    own = own_ref[...]
    got = got_ref[...]
    out_ref[...] = compose(jnp.where(first, got, own), jnp.where(first, own, got))


def join_kernel(core_ref, near_ref, far_ref, out_ref, half_ref):
    out = compose(near_ref[...], far_ref[...])
    out_ref[...] = out
    half_ref[...] = jnp.where(core_ref[0] == 0, out[:, :N], out[:, N:])


def half_kernel(core_ref, near_ref, far_ref, out_ref):
    near = near_ref[...]
    extra = jnp.where(core_ref[0] == 0, 0.0, near[:, N:])
    out_ref[...] = advance(near[:, :N], far_ref[...], extra)


def finish_kernel(core_ref, r0_ref, hi_ref, lo_ref, own_ref, swap_ref, far0_ref, far1_ref, first_ref, gate_ref, out_ref):
    first = core_ref[0] == 0
    own = own_ref[...]
    swap = swap_ref[...]
    state = advance(
        jnp.where(first, own, swap), far0_ref[...] + far1_ref[...], jnp.where(first, swap, own)
    )
    state = jnp.where(first, state, advance(first_ref[:, :N], state, first_ref[:, N:]))
    y_both = lanes(*split2(state))
    y_both = rows(y_both, y_both)
    for b in range(r0_ref.shape[0]):
        both = dot(lanes(hi_ref[b], lo_ref[b]), y_both)
        res = r0_ref[b] + both[:, :N] + both[:, N:]
        norm = lax.rsqrt(jnp.mean(res * res, axis=1, keepdims=True) + EPS)
        out_ref[b] = (res * norm * gate_ref[b]).astype(BF16)


def call(kernel, out_shape, inputs, core=None, remote=(), spill=(), sems=0):
    vmem = pl.BlockSpec(memory_space=pltpu.VMEM)
    hbm = pl.BlockSpec(memory_space=pltpu.HBM)
    specs = [vmem] * len(inputs) + [hbm] * len(remote)
    inputs = [*inputs, *(pltpu.with_memory_space_constraint(a, pltpu.HBM) for a in remote)]
    if core is not None:
        specs = [pl.BlockSpec(memory_space=pltpu.SMEM)] + specs
        inputs = [core, *inputs]
    return pl.pallas_call(
        kernel,
        out_shape=[*out_shape, *(pltpu.HBM(o.shape, o.dtype) for o in spill)],
        in_specs=specs,
        out_specs=[vmem] * len(out_shape) + [hbm] * len(spill),
        scratch_shapes=[pltpu.VMEM(o.shape, o.dtype) for o in (*remote, *spill)]
        + ([pltpu.SemaphoreType.DMA((sems,))] if sems else []),
        compiler_params=pltpu.CompilerParams(vmem_limit_bytes=40 * 2**20),
    )(*inputs)


def near(*arrays):
    return [pltpu.with_memory_space_constraint(a, pltpu.VMEM) for a in arrays]


def kept(*dims, dtype=F32):
    return pltpu.VMEM(dims, dtype)


def shape(*dims, dtype=F32):
    return jax.ShapeDtypeStruct(dims, dtype)


def by_head(array):
    return jnp.transpose(array, (1, 0, 2))


def to_heads(array):
    return lax.all_to_all(array, "head", split_axis=0, concat_axis=0, tiled=True)


def layer(queries, keys, values, beta, log_decay, out_gate, norm_gain):
    tokens, heads, _ = values.shape
    z = lax.axis_size("z")
    flat = lambda array: array.reshape(tokens * heads, N)
    (kv,) = call(
        pack_kernel,
        [kept(heads, tokens + 8, 2 * N, dtype=BF16)],
        [flat(keys), flat(values), beta, log_decay],
    )
    kv = to_heads(kv)
    qg = jnp.concatenate([by_head(queries), by_head(out_gate)], axis=2)
    blocks = kv.shape[0]
    square = kept(N, N)
    wide = kept(N, 2 * N)
    wide16 = shape(blocks, N, 2 * N, dtype=BF16)
    core = lax.axis_index("c").astype(jnp.int32).reshape(1)
    kv, qg = lax.optimization_barrier((kv, qg))
    total, en, wu_hi, wu_lo, grow, nodes = call(
        terms_kernel,
        [wide],
        near(kv),
        spill=[
            shape(blocks, N, N),
            wide16,
            wide16,
            shape(blocks, 8, N),
            shape(blocks - 1, N, 2 * N),
        ],
        sems=8,
    )
    got = lax.ppermute(total, "c", [(0, 1), (1, 0)])
    (window,) = call(pair_kernel, [wide], near(total, got), core)

    def up(x, d):
        return lax.ppermute(x, "z", [(i, i + d) for i in range(z - d)])

    def cross(x, d, *routes):
        pairs = [
            (2 * i + source, 2 * (i + d) + target)
            for i in range(z - d)
            for source, target in zip(routes[::2], routes[1::2])
        ]
        return lax.ppermute(x, ("z", "c"), pairs)

    span = 1
    while span * 4 < z:
        window, half = call(join_kernel, [wide, square], near(window, up(window, span)), core)
        span *= 2
    far = up(half, span)
    qg, half = lax.optimization_barrier((qg, half))
    qg = to_heads(qg)
    (half,) = call(half_kernel, [square], near(window, far), core)
    span *= 2
    own = up(half, 1)
    other = cross(half, 1, 0, 1, 1, 0)
    far0 = cross(half, span + 1, 1, 0)
    far1 = cross(half, span + 1, 1, 1)
    cube = kept(blocks, N, N)
    cube16 = kept(blocks, N, N, dtype=BF16)
    r0, r1_hi, r1_lo, gate = call(
        reach_kernel,
        [cube, cube16, cube16, cube],
        [*near(kv, qg), norm_gain.reshape(1, N)],
        remote=[en, wu_hi, wu_lo, grow, nodes],
        sems=5,
    )
    (out,) = call(
        finish_kernel,
        [shape(blocks, N, N, dtype=BF16)],
        near(r0, r1_hi, r1_lo, own, other, far0, far1, got, gate),
        core,
    )
    return out.reshape(blocks * N, 1, N)


def solution(mesh):
    finer = Mesh(mesh.devices.reshape(-1, 2, mesh.shape["head"]), ("z", "c", "head"))
    tokens = ("z", "c", "head")
    in_specs = (
        P(tokens, None, None),
        P(tokens, None, None),
        P(tokens, None, None),
        P(tokens, None),
        P(tokens, None),
        P(tokens, None, None),
        P(),
    )
    out_specs = P(("z", "c"), "head", None)
    return jax.shard_map(layer, mesh=finer, in_specs=in_specs, out_specs=out_specs, check_vma=False)
```

time: 109 us -> 103 us (0.945)
  the two profiles are of different devices: /device:TPU:34 before, /device:TPU:2 now
where the time goes in v2:
time: 103 us; the launch traced here: 102 us
  starting transfers between devices  59.2 us (57%)
  waiting for transfers between devices  22.4 us (22%)
  Pallas kernels  15.6 us (15%)
  local copies, waits for them, and re-layouts  3.95 us (4%)
  other arithmetic  1.12 us (1%)
    ppermute x4, starting transfers between devices, up(): return lax.ppermute(x, 'z', [(i, i + d) for i in range(z - d)])  26.7 us
    ppermute x3, starting transfers between devices, cross(): return lax.ppermute(x, ('z', 'c'), pairs)  15.7 us
    pallas_call x8, Pallas kernels, call(): pl.pallas_call(kernel, out_shape=[*out_shape, *(pltpu.HBM(o.shape, o.dtyp...  15.6 us
    all_to_all x2, starting transfers between devices, to_heads(): lax.all_to_all(array, 'head', split_axis=0, concat_axis=0, tiled=True)  14.9 us
    all_to_all x2, waiting for transfers between devices, to_heads(): lax.all_to_all(array, 'head', split_axis=0, concat_axis=0, tiled=True)  13.7 us
    ppermute x4, waiting for transfers between devices, up(): return lax.ppermute(x, 'z', [(i, i + d) for i in range(z - d)])  7.43 us
    unnamed x12, local copies, waits for them, and re-layouts  3.68 us
  transfers between devices with their start and end apart: 10, of which 5 were waited for; matrix products, arithmetic and copies ran while one was open for 1% of the time, Pallas kernels for 4%

profile of v2, /device:TPU:2, one launch (start us, length us, event | category | flops | bytes accessed | tf_op | source)
XLA Modules:
  0.0 102.4 jit_solution(15796595079296289981)
XLA Ops:
  0.0 0.8 copy.8.beta_ref
  0.8 0.8 copy.9.decay_ref
  1.6 1.0 %copy-done = bf16[128,16,128]{2,1,0:T(8,128)(2,1)S(1)} copy-done((bf16[128,16,128]{2,1,0:T(8,128)(2,1)S(1)}, bf16[128,16,128]{2,1,0:T(8,128)(2,1)}, u32[]{:S(2)}) %copy-start) | copy-done | bytes 524312
  2.6 1.0 %copy-done.1 = bf16[128,16,128]{2,1,0:T(8,128)(2,1)S(1)} copy-done((bf16[128,16,128]{2,1,0:T(8,128)(2,1)S(1)}, bf16[128,16,128]{2,1,0:T(8,128)(2,1)}, u32[]{:S(2)}) %copy-start.1) | copy-done | bytes 524312
  3.7 1.5 %shard_map.73 = bf16[16,136,256]{2,1,0:T(8,128)(2,1)} custom-call(bf16[2048,128]{1,0:T(8,128)(2,1)S(1)} %bitcast.9, bf16[2048,128]{1,0:T(8,128)(2,1)S(1)} %bitcast.10, f32[128,16]{1,0:T(8,128)S(1)} %copy.8.beta_ref, f32[128,16]{1,0:T(8,128)S(1)} %copy.9.decay_ref), custom_call_target="tpu_custom_call" | custom-call | tf_op jit(solution)/shard_map/pallas_call | solution.py:272
  5.1 9.4 %all-to-all-start = ((bf16[16,136,256]{2,1,0:T(8,128)(2,1)}), bf16[16,136,256]{2,1,0:T(8,128)(2,1)S(1)}, u32[]{:S(2)}, u32[]{:S(2)}) async-start(bf16[16,136,256]{2,1,0:T(8,128)(2,1)} %shard_map.73), calls=%async_computation | async-start | bytes 2228224 | tf_op jit(solution)/shard_map/all_to_all | solution.py:300
  14.8 1.1 %pad_maximum_fusion = bf16[16,128,256]{2,1,0:T(8,128)(2,1)} fusion(bf16[16,128,128]{2,1,0:T(8,128)(2,1)S(1)} %get-tuple-element.37, bf16[16,128,128]{2,1,0:T(8,128)(2,1)S(1)} %get-tuple-element.38), kind=kLoop, calls=%fused_computation | loop fusion | flops 2097152 | bytes 2097152 | tf_op jit(solution)/shard_map/concatenate | solution.py:313
  15.9 13.7 %all-to-all-done.kv_ref = bf16[16,136,256]{2,1,0:T(8,128)(2,1)S(1)} async-done(((bf16[16,136,256]{2,1,0:T(8,128)(2,1)}), bf16[16,136,256]{2,1,0:T(8,128)(2,1)S(1)}, u32[]{:S(2)}, u32[]{:S(2)}) %all-to-all-start) | async-done | bytes 1114144 | tf_op jit(solution)/shard_map/all_to_all | solution.py:300
  29.6 7.1 %shard_map.74 = (f32[128,256]{1,0:T(8,128)S(1)}, f32[16,128,128]{2,1,0:T(8,128)}, bf16[16,128,256]{2,1,0:T(8,128)(2,1)}, bf16[16,128,256]{2,1,0:T(8,128)(2,1)}, ...) custom-call(bf16[16,136,256]{2,1,0:T(8,128)(2,1)S(1)} %all-to-all-done.kv_ref), custom_call_target="tpu_custom_call" | custom-call | tf_op jit(solution)/shard_map/pallas_call | solution.py:272
  36.7 1.9 %collective-permute-start = (f32[128,256]{1,0:T(8,128)S(1)}, f32[128,256]{1,0:T(8,128)S(1)}, u32[]{:S(2)}, u32[]{:S(2)}) collective-permute-start(f32[128,256]{1,0:T(8,128)S(1)} %get-tuple-element.23.own_ref), channel_id=1, source_target_pairs={{0,16},{16,0},{1,17},{17,1},{2,18},{18,2},{3,19},{19,3},{4,20},{20... | collective-permute-start | bytes 393224 | tf_op jit(solution)/shard_map/ppermute | solution.py:333
  38.7 1.3 %collective-permute-done.got_ref.first_ref = f32[128,256]{1,0:T(8,128)S(1)} collective-permute-done((f32[128,256]{1,0:T(8,128)S(1)}, f32[128,256]{1,0:T(8,128)S(1)}, u32[]{:S(2)}, u32[]{:S(2)}) %collective-permute-start) | collective-permute-done | bytes 131104 | tf_op jit(solution)/shard_map/ppermute | solution.py:333
  40.2 3.3 %collective-permute-start.1 = (f32[128,256]{1,0:T(8,128)S(1)}, f32[128,256]{1,0:T(8,128)S(1)}, u32[]{:S(2)}, u32[]{:S(2)}) collective-permute-start(f32[128,256]{1,0:T(8,128)S(1)} %shard_map.75.near_ref), channel_id=1, source_target_pairs={{0,32},{32,64},{64,96},{96,128},{128,160},{160,192},{192,224},{224... | collective-permute-start | bytes 393224 | tf_op jit(solution)/shard_map/ppermute | solution.py:337
  43.5 3.0 %collective-permute-done.1.far_ref = f32[128,256]{1,0:T(8,128)S(1)} collective-permute-done((f32[128,256]{1,0:T(8,128)S(1)}, f32[128,256]{1,0:T(8,128)S(1)}, u32[]{:S(2)}, u32[]{:S(2)}) %collective-permute-start.1) | collective-permute-done | bytes 131104 | tf_op jit(solution)/shard_map/ppermute | solution.py:337
  46.6 0.8 shard_map.76
  47.4 5.7 %collective-permute-start.2 = (f32[128,256]{1,0:T(8,128)S(1)}, f32[128,256]{1,0:T(8,128)S(1)}, u32[]{:S(2)}, u32[]{:S(2)}) collective-permute-start(f32[128,256]{1,0:T(8,128)S(1)} %get-tuple-element.24.near_ref), channel_id=1, source_target_pairs={{0,64},{32,96},{64,128},{96,160},{128,192},{160,224},{192,256},{22... | collective-permute-start | bytes 393224 | tf_op jit(solution)/shard_map/ppermute | solution.py:337
  53.1 2.5 %collective-permute-done.2.far_ref = f32[128,256]{1,0:T(8,128)S(1)} collective-permute-done((f32[128,256]{1,0:T(8,128)S(1)}, f32[128,256]{1,0:T(8,128)S(1)}, u32[]{:S(2)}, u32[]{:S(2)}) %collective-permute-start.2) | collective-permute-done | bytes 131104 | tf_op jit(solution)/shard_map/ppermute | solution.py:337
  55.8 5.5 %all-to-all-start.1 = ((bf16[16,128,256]{2,1,0:T(8,128)(2,1)}), bf16[16,128,256]{2,1,0:T(8,128)(2,1)S(1)}, u32[]{:S(2)}, u32[]{:S(2)}) async-start(bf16[16,128,256]{2,1,0:T(8,128)(2,1)} %pad_maximum_fusion), calls=%async_computation.1 | async-start | bytes 2097152 | tf_op jit(solution)/shard_map/all_to_all | solution.py:300
  61.3 13.6 %collective-permute-start.3 = (f32[128,128]{1,0:T(8,128)S(1)}, f32[128,128]{1,0:T(8,128)S(1)}, u32[]{:S(2)}, u32[]{:S(2)}) collective-permute-start(f32[128,128]{1,0:T(8,128)S(1)} %get-tuple-element.25), channel_id=1, source_target_pairs={{0,128},{32,160},{64,192},{96,224},{128,256},{160,288},{192,320},{... | collective-permute-start | bytes 196616 | tf_op jit(solution)/shard_map/ppermute | solution.py:337
  74.9 1.9 %collective-permute-done.3.far_ref = f32[128,128]{1,0:T(8,128)S(1)} collective-permute-done((f32[128,128]{1,0:T(8,128)S(1)}, f32[128,128]{1,0:T(8,128)S(1)}, u32[]{:S(2)}, u32[]{:S(2)}) %collective-permute-start.3) | collective-permute-done | bytes 65568 | tf_op jit(solution)/shard_map/ppermute | solution.py:337
  77.0 0.7 collective-permute-start.7
  78.3 14.4 %collective-permute-start.5 = (f32[128,128]{1,0:T(8,128)S(1)}, f32[128,128]{1,0:T(8,128)S(1)}, u32[]{:S(2)}, u32[]{:S(2)}) collective-permute-start(f32[128,128]{1,0:T(8,128)S(1)} %shard_map.79), channel_id=1, source_target_pairs={{0,48},{16,32},{32,80},{48,64},{64,112},{80,96},{96,144},{112,128}... | collective-permute-start | bytes 196616 | tf_op jit(solution)/shard_map/ppermute | solution.py:345
  92.7 4.0 %collective-permute-start.4 = (f32[128,128]{1,0:T(8,128)S(1)}, f32[128,128]{1,0:T(8,128)S(1)}, u32[]{:S(2)}, u32[]{:S(2)}) collective-permute-start(f32[128,128]{1,0:T(8,128)S(1)} %shard_map.79), channel_id=1, source_target_pairs={{0,32},{32,64},{64,96},{96,128},{128,160},{160,192},{192,224},{224... | collective-permute-start | bytes 196616 | tf_op jit(solution)/shard_map/ppermute | solution.py:337
  96.7 3.9 %shard_map.78 = (f32[16,128,128]{2,1,0:T(8,128)S(1)}, bf16[16,128,128]{2,1,0:T(8,128)(2,1)S(1)}, bf16[16,128,128]{2,1,0:T(8,128)(2,1)S(1)}, f32[16,128,128]{2,1,0:T(8,128)S(1)}) custom-call(bf16[16,136,256]{2,1,0:T(8,128)(2,1)S(1)} %all-to-all-done.kv_ref, bf16[16,128,256]{2,1,0:T(8,128)(2,1)S(1)} %all-to-all-done.1.qg_ref, f32[1,128]{1,0:T(1,128)S(1)} %bitcast.11, ...), custom_call_target="tpu_custom_call" | custom-call | tf_op jit(solution)/shard_map/pallas_call | solution.py:272
  100.7 1.7 %shard_map.80 = bf16[16,128,128]{2,1,0:T(8,128)(2,1)} custom-call(s32[1]{0:T(128)} %bitcast.core_ref, f32[16,128,128]{2,1,0:T(8,128)S(1)} %get-tuple-element.32.r0_ref, bf16[16,128,128]{2,1,0:T(8,128)(2,1)S(1)} %get-tuple-element.33.hi_ref, bf16[16,128,128]{2,1,0:T(8,128)(2,1)S(1)} %get-tuple-element.34.lo_ref, ...), custom_call_target="tpu_custom_call" | custom-call | tf_op jit(solution)/shard_map/pallas_call | solution.py:272
  (18 shorter events, 1.5 us)
Async XLA Ops:
  1.6 1.0 %copy-start = (bf16[128,16,128]{2,1,0:T(8,128)(2,1)S(1)}, bf16[128,16,128]{2,1,0:T(8,128)(2,1)}, u32[]{:S(2)}) copy-start(bf16[128,16,128]{2,1,0:T(8,128)(2,1)} %param.8) | copy-start | bytes 1572868
  2.6 1.0 %copy-start.1 = (bf16[128,16,128]{2,1,0:T(8,128)(2,1)S(1)}, bf16[128,16,128]{2,1,0:T(8,128)(2,1)}, u32[]{:S(2)}) copy-start(bf16[128,16,128]{2,1,0:T(8,128)(2,1)} %param.9) | copy-start | bytes 1572868
  3.7 10.8 %copy-start.3 = (bf16[128,16,128]{2,1,0:T(8,128)(2,1)S(1)}, bf16[128,16,128]{2,1,0:T(8,128)(2,1)}, u32[]{:S(2)}) copy-start(bf16[128,16,128]{2,1,0:T(8,128)(2,1)} %param.12) | copy-start | bytes 1572868
  3.7 10.8 %copy-start.4 = (bf16[128,16,128]{2,1,0:T(8,128)(2,1)S(1)}, bf16[128,16,128]{2,1,0:T(8,128)(2,1)}, u32[]{:S(2)}) copy-start(bf16[128,16,128]{2,1,0:T(8,128)(2,1)} %param.7) | copy-start | bytes 1572868
  5.1 24.4 %all-to-all-start = ((bf16[16,136,256]{2,1,0:T(8,128)(2,1)}), bf16[16,136,256]{2,1,0:T(8,128)(2,1)S(1)}, u32[]{:S(2)}, u32[]{:S(2)}) async-start(bf16[16,136,256]{2,1,0:T(8,128)(2,1)} %shard_map.73), calls=%async_computation | async-start | bytes 2228224 | tf_op jit(solution)/shard_map/all_to_all | solution.py:300
  15.9 80.8 %copy-start.2 = (f32[128]{0:T(128)S(1)}, f32[128]{0:T(128)}, u32[]{:S(2)}) copy-start(f32[128]{0:T(128)} %param.13) | copy-start | bytes 1540
  36.7 3.2 %collective-permute-start = (f32[128,256]{1,0:T(8,128)S(1)}, f32[128,256]{1,0:T(8,128)S(1)}, u32[]{:S(2)}, u32[]{:S(2)}) collective-permute-start(f32[128,256]{1,0:T(8,128)S(1)} %get-tuple-element.23.own_ref), channel_id=1, source_target_pairs={{0,16},{16,0},{1,17},{17,1},{2,18},{18,2},{3,19},{19,3},{4,20},{20... | collective-permute-start | bytes 393224 | tf_op jit(solution)/shard_map/ppermute | solution.py:333
  40.2 6.4 %collective-permute-start.1 = (f32[128,256]{1,0:T(8,128)S(1)}, f32[128,256]{1,0:T(8,128)S(1)}, u32[]{:S(2)}, u32[]{:S(2)}) collective-permute-start(f32[128,256]{1,0:T(8,128)S(1)} %shard_map.75.near_ref), channel_id=1, source_target_pairs={{0,32},{32,64},{64,96},{96,128},{128,160},{160,192},{192,224},{224... | collective-permute-start | bytes 393224 | tf_op jit(solution)/shard_map/ppermute | solution.py:337
  47.4 8.2 %collective-permute-start.2 = (f32[128,256]{1,0:T(8,128)S(1)}, f32[128,256]{1,0:T(8,128)S(1)}, u32[]{:S(2)}, u32[]{:S(2)}) collective-permute-start(f32[128,256]{1,0:T(8,128)S(1)} %get-tuple-element.24.near_ref), channel_id=1, source_target_pairs={{0,64},{32,96},{64,128},{96,160},{128,192},{160,224},{192,256},{22... | collective-permute-start | bytes 393224 | tf_op jit(solution)/shard_map/ppermute | solution.py:337
  55.8 40.9 %all-to-all-start.1 = ((bf16[16,128,256]{2,1,0:T(8,128)(2,1)}), bf16[16,128,256]{2,1,0:T(8,128)(2,1)S(1)}, u32[]{:S(2)}, u32[]{:S(2)}) async-start(bf16[16,128,256]{2,1,0:T(8,128)(2,1)} %pad_maximum_fusion), calls=%async_computation.1 | async-start | bytes 2097152 | tf_op jit(solution)/shard_map/all_to_all | solution.py:300
  61.3 15.5 %collective-permute-start.3 = (f32[128,128]{1,0:T(8,128)S(1)}, f32[128,128]{1,0:T(8,128)S(1)}, u32[]{:S(2)}, u32[]{:S(2)}) collective-permute-start(f32[128,128]{1,0:T(8,128)S(1)} %get-tuple-element.25), channel_id=1, source_target_pairs={{0,128},{32,160},{64,192},{96,224},{128,256},{160,288},{192,320},{... | collective-permute-start | bytes 196616 | tf_op jit(solution)/shard_map/ppermute | solution.py:337
  77.0 23.7 %collective-permute-start.7 = (f32[128,128]{1,0:T(8,128)S(1)}, f32[128,128]{1,0:T(8,128)S(1)}, u32[]{:S(2)}, u32[]{:S(2)}) collective-permute-start(f32[128,128]{1,0:T(8,128)S(1)} %shard_map.79), channel_id=1, source_target_pairs={{16,304},{48,336},{80,368},{112,400},{144,432},{176,464},{208,496}... | collective-permute-start | bytes 196616 | tf_op jit(solution)/shard_map/ppermute | solution.py:345
  77.6 23.0 %collective-permute-start.6 = (f32[128,128]{1,0:T(8,128)S(1)}, f32[128,128]{1,0:T(8,128)S(1)}, u32[]{:S(2)}, u32[]{:S(2)}) collective-permute-start(f32[128,128]{1,0:T(8,128)S(1)} %shard_map.79), channel_id=1, source_target_pairs={{16,288},{48,320},{80,352},{112,384},{144,416},{176,448},{208,480}... | collective-permute-start | bytes 196616 | tf_op jit(solution)/shard_map/ppermute | solution.py:345
  78.3 22.4 %collective-permute-start.5 = (f32[128,128]{1,0:T(8,128)S(1)}, f32[128,128]{1,0:T(8,128)S(1)}, u32[]{:S(2)}, u32[]{:S(2)}) collective-permute-start(f32[128,128]{1,0:T(8,128)S(1)} %shard_map.79), channel_id=1, source_target_pairs={{0,48},{16,32},{32,80},{48,64},{64,112},{80,96},{96,144},{112,128}... | collective-permute-start | bytes 196616 | tf_op jit(solution)/shard_map/ppermute | solution.py:345
  92.7 8.0 %collective-permute-start.4 = (f32[128,128]{1,0:T(8,128)S(1)}, f32[128,128]{1,0:T(8,128)S(1)}, u32[]{:S(2)}, u32[]{:S(2)}) collective-permute-start(f32[128,128]{1,0:T(8,128)S(1)} %shard_map.79), channel_id=1, source_target_pairs={{0,32},{32,64},{64,96},{96,128},{128,160},{160,192},{192,224},{224... | collective-permute-start | bytes 196616 | tf_op jit(solution)/shard_map/ppermute | solution.py:337
